TPU v7x, 32 devices: a whole 2x2x4 slice. The times are simulated.
32 devices in a mesh: row: 4 (over z), col: 4 (over x, core), depth: 2 (over y).
Axes of the slice: x: 2, y: 2, z: 4, core: 2. Of those that a mesh axis runs over, the one named last changes fastest.
Arguments:
- tokens: bfloat16 [2048, 8192], P(('row', 'col'), 'depth'), may hold values from -0.3125 to 0.3125
- weight: bfloat16 [8192, 8192], P('depth', ('col', 'row')), may hold values from -0.0625 to 0.0625
- grad_output: bfloat16 [2048, 8192], P('row', ('col', 'depth')), may hold values from -6 to 6
Outputs:
- grad_input: bfloat16 [2048, 8192], P(('row', 'col'), 'depth')
- grad_weight: bfloat16 [8192, 8192], P('depth', ('col', 'row'))
All inputs are finite; a program needn't handle non-finite values.
Results may differ from a plain program's by a relative error of at most 0.001.
Values may be sent and summed in bfloat16 or wider, within the bound.
A program may use at most 128 MiB of HBM per device.

v0:
```python
import jax
import jax.numpy as jnp
from jax import lax
from jax.sharding import PartitionSpec as P

last_with_last = (((1,), (1,)), ((), ()))
first_with_first = (((0,), (0,)), ((), ()))


def input_grads(weight, grad_block):
    weight_block = lax.all_gather(weight, "row", axis=1, tiled=True)
    partial_value = lax.dot_general(
        grad_block, weight_block, last_with_last, preferred_element_type=jnp.float32
    )
    column_slab = lax.psum_scatter(partial_value, "col", scatter_dimension=1, tiled=True).astype(
        jnp.bfloat16
    )
    return lax.all_to_all(column_slab, "col", split_axis=0, concat_axis=1, tiled=True)


def weight_grads(tokens, grad_block):
    partial_value = lax.dot_general(
        lax.all_gather(tokens, "col", axis=0, tiled=True),
        grad_block,
        first_with_first,
        preferred_element_type=jnp.float32,
    )
    return lax.psum_scatter(partial_value, "row", scatter_dimension=1, tiled=True).astype(
        jnp.bfloat16
    )


def per_device(tokens, weight, grad_output):
    grad_block = lax.all_gather(grad_output, "depth", axis=1, tiled=True)
    grad_input = input_grads(weight, grad_block)
    grad_weight = weight_grads(tokens, grad_block)
    return (grad_input, grad_weight)


def solution(mesh):
    return jax.shard_map(
        per_device,
        mesh=mesh,
        in_specs=(
            P(("row", "col"), "depth"),
            P("depth", ("col", "row")),
            P("row", ("col", "depth")),
        ),
        out_specs=(P(("row", "col"), "depth"), P("depth", ("col", "row"))),
        check_vma=False,
    )
```

profile of v0, /device:TPU:0, one launch (start us, length us, event | category | flops | bytes accessed | tf_op | source)
XLA Modules:
  0.0 1008.6 jit_solution(7018529357525210481)
XLA Ops:
  7.2 0.0 all-gather.4.cloned.1.call-start
  7.2 0.7 all-gather.4.cloned.1.call-update
  7.9 0.0 all-gather.6.cloned.1.call-start
  7.9 0.7 all-gather.6.cloned.1.call-update
  8.6 0.0 all-gather.8.cloned.1.call-start
  8.7 0.7 all-gather.8.cloned.1.call-update
  9.4 0.0 reduce-scatter.3.cloned.1.call-start
  9.4 35.9 %all-gather.4.cloned.1.call-done = bf16[512,2048]{1,0:T(8,128)(2,1)} async-done(((bf16[512,1024]{1,0:T(8,128)(2,1)}), bf16[512,2048]{1,0:T(8,128)(2,1)}) %all-gather.4.cloned.1.call-update) | async-done | bytes 2097168 | tf_op jit(solution)/shard_map/all_gather | solution.py:34
  45.4 288.4 %all-gather.6.cloned.1.call-done = bf16[4096,2048]{1,0:T(8,128)(2,1)} async-done(((bf16[4096,512]{1,0:T(8,128)(2,1)}), bf16[4096,2048]{1,0:T(8,128)(2,1)}) %all-gather.6.cloned.1.call-update) | async-done | bytes 16777232 | tf_op jit(solution)/shard_map/all_gather | solution.py:11
  333.7 15.1 %fusion = f32[512,4096]{1,0:T(8,128)} fusion(bf16[512,2048]{1,0:T(8,128)(2,1)} %all-gather.4.cloned.1.call-done, bf16[4096,2048]{1,0:T(8,128)(2,1)} %all-gather.6.cloned.1.call-done), kind=kOutput, calls=%fused_computation | convolution fusion | flops 8589934592 | bytes 27262976 | tf_op jit(solution)/shard_map/dot_general | solution.py:12
  348.8 0.0 copy-start
  348.8 0.0 reduce-scatter.3.cloned.1.call-update
  348.8 0.0 reduce-scatter.5.cloned.1.call-start
  348.9 19.1 %all-gather.8.cloned.1.call-done = bf16[512,4096]{1,0:T(8,128)(2,1)} async-done(((bf16[128,4096]{1,0:T(8,128)(2,1)}), bf16[512,4096]{1,0:T(8,128)(2,1)}) %all-gather.8.cloned.1.call-update) | async-done | bytes 4194320 | tf_op jit(solution)/shard_map/all_gather | solution.py:23
  368.0 0.0 copy-done
  368.0 21.6 %fusion.1 = f32[4096,2048]{1,0:T(8,128)} fusion(bf16[512,4096]{1,0:T(8,128)(2,1)} %all-gather.8.cloned.1.call-done, bf16[512,2048]{1,0:T(8,128)(2,1)S(1)} %copy-done), kind=kOutput, calls=%fused_computation.1 | convolution fusion | flops 8589934592 | bytes 39845888 | tf_op jit(solution)/shard_map/dot_general | solution.py:22
  389.5 0.0 reduce-scatter.5.cloned.1.call-update
  389.6 52.2 %reduce-scatter.3.cloned.1.call-done = f32[512,1024]{1,0:T(8,128)} async-done(((f32[512,4096]{1,0:T(8,128)}), f32[512,1024]{1,0:T(8,128)}) %reduce-scatter.3.cloned.1.call-update) | async-done | bytes 2097168 | tf_op jit(solution)/shard_map/reduce_scatter | solution.py:15
  441.7 1.7 convert_element_type.6
  443.5 16.9 %all_to_all.19 = bf16[4,128,1024]{2,1,0:T(8,128)(2,1)S(1)} all-to-all(bf16[4,128,1024]{2,1,0:T(8,128)(2,1)S(1)} %bitcast.8), channel_id=1, replica_groups=mesh['row'=4,'col'=4,'depth'=2] {'col'}, dimensions={0} | all-to-all | bytes 2097152 | tf_op jit(solution)/shard_map/all_to_all | solution.py:18
  460.3 1.1 copy.6
  461.4 534.8 %reduce-scatter.5.cloned.1.call-done = f32[4096,512]{1,0:T(8,128)} async-done(((f32[4096,2048]{1,0:T(8,128)}), f32[4096,512]{1,0:T(8,128)}) %reduce-scatter.5.cloned.1.call-update) | async-done | bytes 8388624 | tf_op jit(solution)/shard_map/reduce_scatter | solution.py:28
  996.1 5.9 convert_element_type.7
Async XLA Ops:
  7.2 38.2 %all-gather.4.cloned.1.call-start = ((), (), s32[]{:S(2)}) async-start(), calls=%async_computation.3 | async-start | bytes 3145728 | tf_op jit(solution)/shard_map/all_gather | solution.py:34
  7.9 325.8 %all-gather.6.cloned.1.call-start = ((), (), s32[]{:S(2)}) async-start(), calls=%async_computation.4 | async-start | bytes 20971520 | tf_op jit(solution)/shard_map/all_gather | solution.py:11
  8.6 359.3 %all-gather.8.cloned.1.call-start = ((), (), s32[]{:S(2)}) async-start(), calls=%async_computation.6 | async-start | bytes 5242880 | tf_op jit(solution)/shard_map/all_gather | solution.py:23
  9.4 432.3 %reduce-scatter.3.cloned.1.call-start = ((), (), s32[]{:S(2)}) async-start(), calls=%async_computation.5 | async-start | bytes 10485760 | tf_op jit(solution)/shard_map/reduce_scatter | solution.py:15
  348.8 19.2 %copy-start = (bf16[512,2048]{1,0:T(8,128)(2,1)S(1)}, bf16[512,2048]{1,0:T(8,128)(2,1)}, u32[]{:S(2)}) copy-start(bf16[512,2048]{1,0:T(8,128)(2,1)} %all-gather.4.cloned.1.call-done) | copy-start | bytes 6291460
  348.8 647.3 %reduce-scatter.5.cloned.1.call-start = ((), (), s32[]{:S(2)}) async-start(), calls=%async_computation.7 | async-start | bytes 41943040 | tf_op jit(solution)/shard_map/reduce_scatter | solution.py:28
Sparse Core Ops, SparseCore 0:
  9.5 35.8 all-gather.3
  46.9 286.7 all-gather.5
  335.3 32.6 all-gather.7
  370.4 71.2 reduce-scatter.2
  443.9 552.1 reduce-scatter.4
where the time goes:
time: 1010 us
  waiting for transfers between devices  932 us (92%)
  matrix products  36.6 us (4%)
  blocking collectives  16.9 us (2%)
  between operations  13.8 us (1%)
    reduce_scatter x1, waiting for transfers between devices, weight_grads(): lax.psum_scatter(partial_value, 'row', scatter_dimension=1, tiled=True)  535 us
    all_gather x1, waiting for transfers between devices, input_grads(): weight_block = lax.all_gather(weight, 'row', axis=1, tiled=True)  288 us
    reduce_scatter x1, waiting for transfers between devices, input_grads(): lax.psum_scatter(partial_value, 'col', scatter_dimension=1, tiled=True)  52.2 us
    all_gather x1, waiting for transfers between devices, per_device(): grad_block = lax.all_gather(grad_output, 'depth', axis=1, tiled=True)  35.9 us
    dot_general x1, matrix products, weight_grads(): lax.dot_general(lax.all_gather(tokens, 'col', axis=0, tiled=True), grad_b...  21.6 us
  transfers between devices with their start and end apart: 5, of which 5 were waited for; matrix products, arithmetic and copies ran while one was open for 4% of the time, Pallas kernels for 0%

commit v1 on v0

--- a/solution.py
+++ b/solution.py
@@ -3,8 +3,10 @@
 from jax import lax
 from jax.sharding import PartitionSpec as P
 
+
 last_with_last = (((1,), (1,)), ((), ()))
 first_with_first = (((0,), (0,)), ((), ()))
+CHUNKS = 4
 
 
 def input_grads(weight, grad_block):
@@ -30,16 +32,121 @@
     )
 
 
-def per_device(tokens, weight, grad_output):
+def per_device_general(tokens, weight, grad_output):
     grad_block = lax.all_gather(grad_output, "depth", axis=1, tiled=True)
     grad_input = input_grads(weight, grad_block)
     grad_weight = weight_grads(tokens, grad_block)
     return (grad_input, grad_weight)
 
 
+def along_row(value, step):
+    return lax.ppermute(value, "row", [(i, (i + step) % 4) for i in range(4)])
+
+
+def next_row(value, sign, reach):
+    pairs = [(i, i + 1) for i in range(4 - reach)]
+    return lax.ppermute(value, "row", pairs if sign > 0 else [(3 - i, 3 - j) for i, j in pairs])
+
+
+def across_col(value, bits):
+    return lax.ppermute(value, "col", [(i, i ^ bits) for i in range(4)])
+
+
+def gather_row(block, row):
+    up, down = [block], [block]
+    for step in (1, 2, 3):
+        sources = range(step - 1, 3)
+        up.append(lax.ppermute(up[-1], "row", [(i, i + 1) for i in sources]))
+        down.append(lax.ppermute(down[-1], "row", [(3 - i, 2 - i) for i in sources]))
+    return [block] + [jnp.where(row >= s, up[s], down[4 - s]) for s in (1, 2, 3)]
+
+
+def scatter_row(terms):
+    up = next_row(terms[1], 1, 3)
+    down = next_row(terms[3], -1, 3)
+    up = next_row(terms[2] + up, 1, 2)
+    down = next_row(terms[2] + down, -1, 2)
+    up = next_row(terms[3] + up, 1, 1)
+    down = next_row(terms[1] + down, -1, 1)
+    return terms[0] + up + down
+
+
+def per_device_fours(tokens, weight, grad_output):
+    return fours(tokens, weight, grad_output)
+
+
+def fours(tokens, weight, grad_output):
+    row, col, depth = lax.axis_index("row"), lax.axis_index("col"), lax.axis_index("depth")
+    rows, width = tokens.shape[0], weight.shape[1]
+
+    size = weight.shape[0] // CHUNKS
+    chunks = []
+    for j in range(CHUNKS):
+        w0 = weight[j * size : (j + 1) * size]
+        w2 = across_col(w0, 2)
+        chunks.append([w0, across_col(w0, 1), w2, across_col(w2, 1)])
+
+    other = lax.ppermute(grad_output, "depth", [(0, 1), (1, 0)])
+    first = depth == 0
+    grad_block = jnp.concatenate(
+        [jnp.where(first, grad_output, other), jnp.where(first, other, grad_output)], axis=1
+    )
+
+    def columns_of(step):
+        at = lax.rem(row + step, 4) * width
+        return lax.dynamic_slice_in_dim(grad_block, at, width, axis=1)
+
+    mine = [columns_of(0)]
+    for s in (1, 2, 3):
+        mine.append(along_row(columns_of(s), s))
+
+    def of_col(bits):
+        at = jnp.bitwise_xor(col, bits) * rows
+        return [lax.dynamic_slice_in_dim(g, at, rows, axis=0) for g in mine]
+
+    by_col = [of_col(bits) for bits in range(4)]
+
+    packed = [jnp.concatenate(blocks) for blocks in by_col]
+    held = [packed[0]]
+    for bits in (1, 2, 3):
+        held.append(across_col(packed[bits], bits))
+    columns = []
+    for chunk in chunks:
+        total = sum(
+            lax.dot_general(g, w, last_with_last, preferred_element_type=jnp.float32)
+            for g, w in zip(held, chunk)
+        )
+        terms = [total[s * rows : (s + 1) * rows] for s in range(4)]
+        columns.append(scatter_row(terms).astype(jnp.bfloat16))
+    grad_input = jnp.concatenate(columns, axis=1)
+
+    blocks = gather_row(tokens, row)
+    near, far = [], []
+    for block in blocks:
+        near.append(across_col(block, 1))
+        block_x = across_col(block, 2)
+        far.append((block_x, across_col(block_x, 1)))
+    groups = (
+        (blocks + near, by_col[0] + by_col[1]),
+        ([v for pair in far[:2] for v in pair], [by_col[b][s] for s in (0, 1) for b in (2, 3)]),
+        ([v for pair in far[2:] for v in pair], [by_col[b][s] for s in (2, 3) for b in (2, 3)]),
+    )
+    total = None
+    for a, g in groups:
+        value = lax.dot_general(
+            jnp.concatenate(a),
+            jnp.concatenate(g),
+            first_with_first,
+            preferred_element_type=jnp.float32,
+        )
+        total = value if total is None else total + value
+    return grad_input, total.astype(jnp.bfloat16)
+
+
 def solution(mesh):
+    fours_fit = mesh.shape["row"] == 4 and mesh.shape["col"] == 4 and mesh.shape["depth"] == 2
     return jax.shard_map(
-        per_device,
+        per_device_fours if fours_fit else per_device_general,
         mesh=mesh,
         in_specs=(
             P(("row", "col"), "depth"),

time: 1010 us -> 417 us (0.41)
  waiting for transfers between devices: 932 us -> 216 us
  starting transfers between devices: 0.19 us -> 140 us
  blocking collectives: 16.9 us -> 0 us
  local copies, waits for them, and re-layouts: 1.07 us -> 13.7 us
  between operations: 13.8 us -> 1.56 us
    reduce_scatter x2 -> x0, waiting for transfers between devices: 587 us -> none  [the longest x1 535 us: weight_grads(): lax.psum_scatter(partial_value, 'row', scatter_dimension=1, tiled=True)]
    all_gather x3 -> x0, waiting for transfers between devices: 343 us -> none  [the longest x1 288 us: input_grads(): weight_block = lax.all_gather(weight, 'row', axis=1, tiled=True)]
    ppermute x0 -> x61, waiting for transfers between devices: none -> 216 us  [the longest x27 97.2 us: across_col(): return lax.ppermute(value, 'col', [(i, i ^ bits) for i in range(4)])]
    ppermute x0 -> x61, starting transfers between devices: none -> 140 us  [the longest x24 97.1 us: next_row(): lax.ppermute(value, 'row', pairs if sign > 0 else [(3 - i, 3 - j) for i,...]
    all_to_all x1 -> x0, blocking collectives: 16.9 us -> none  [input_grads(): lax.all_to_all(column_slab, 'col', split_axis=0, concat_axis=1, tiled=True)]
    dot_general x2 -> x19, matrix products: 36.6 us -> 34.6 us  [the longest x3 20.2 us: fours(): lax.dot_general(jnp.concatenate(a), jnp.concatenate(g), first_with_first,...]
  transfers between devices with their start and end apart: 5 -> 61, of which waited for: 5 -> 15; matrix products, arithmetic and copies ran while one was open for 4% -> 12% of each run, Pallas kernels for 0% -> 0%
where the time goes in v1:
time: 417 us; the launch traced here: 416 us
  waiting for transfers between devices  216 us (52%)
  starting transfers between devices  140 us (34%)
  matrix products  34.6 us (8%)
  local copies, waits for them, and re-layouts  13.7 us (3%)
  other arithmetic  10.4 us (2%)
    ppermute x27, waiting for transfers between devices, across_col(): return lax.ppermute(value, 'col', [(i, i ^ bits) for i in range(4)])  97.2 us
    ppermute x24, starting transfers between devices, next_row(): lax.ppermute(value, 'row', pairs if sign > 0 else [(3 - i, 3 - j) for i,...  97.1 us
    ppermute x3, waiting for transfers between devices, gather_row(): lax.ppermute(down[-1], 'row', [(3 - i, 2 - i) for i in sources])  43 us
    ppermute x24, waiting for transfers between devices, next_row(): lax.ppermute(value, 'row', pairs if sign > 0 else [(3 - i, 3 - j) for i,...  29.8 us
    ppermute x3, waiting for transfers between devices, along_row(): return lax.ppermute(value, 'row', [(i, (i + step) % 4) for i in range(4)])  28.1 us
    dot_general x3, matrix products, fours(): lax.dot_general(jnp.concatenate(a), jnp.concatenate(g), first_with_first,...  20.2 us
    ppermute x1, waiting for transfers between devices, fours(): other = lax.ppermute(grad_output, 'depth', [(0, 1), (1, 0)])  17.7 us
    ppermute x27, starting transfers between devices, across_col(): return lax.ppermute(value, 'col', [(i, i ^ bits) for i in range(4)])  16 us
  transfers between devices with their start and end apart: 61, of which 15 were waited for; matrix products, arithmetic and copies ran while one was open for 12% of the time, Pallas kernels for 0%

profile of v1, /device:TPU:0, one launch (start us, length us, event | category | flops | bytes accessed | tf_op | source)
XLA Modules:
  0.0 415.6 jit_solution(16908684527169721607)
XLA Ops:
  9.5 17.7 %collective-permute-done = bf16[512,1024]{1,0:T(8,128)(2,1)} collective-permute-done((bf16[512,1024]{1,0:T(8,128)(2,1)}, bf16[512,1024]{1,0:T(8,128)(2,1)}, u32[]{:S(2)}, u32[]{:S(2)}) %collective-permute-start) | collective-permute-done | bytes 1048608 | tf_op jit(solution)/shard_map/ppermute | solution.py:89
  37.6 9.9 %collective-permute-done.1 = bf16[512,512]{1,0:T(8,128)(2,1)} collective-permute-done((bf16[512,512]{1,0:T(8,128)(2,1)}, bf16[512,512]{1,0:T(8,128)(2,1)}, u32[]{:S(2)}, u32[]{:S(2)}) %collective-permute-start.1) | collective-permute-done | bytes 524320 | tf_op jit(solution)/shard_map/ppermute | solution.py:43
  50.2 18.1 %collective-permute-done.2 = bf16[512,512]{1,0:T(8,128)(2,1)} collective-permute-done((bf16[512,512]{1,0:T(8,128)(2,1)}, bf16[512,512]{1,0:T(8,128)(2,1)}, u32[]{:S(2)}, u32[]{:S(2)}) %collective-permute-start.2) | collective-permute-done | bytes 524320 | tf_op jit(solution)/shard_map/ppermute | solution.py:43
  79.7 9.3 %collective-permute-done.6 = bf16[512,512]{1,0:T(8,128)(2,1)S(1)} collective-permute-done((bf16[512,512]{1,0:T(8,128)(2,1)S(1)}, bf16[512,512]{1,0:T(8,128)(2,1)S(1)}, u32[]{:S(2)}, u32[]{:S(2)}) %collective-permute-start.6) | collective-permute-done | bytes 524320 | tf_op jit(solution)/shard_map/ppermute | solution.py:52
  97.1 14.3 %collective-permute-done.17 = bf16[1024,512]{1,0:T(8,128)(2,1)S(1)} collective-permute-done((bf16[1024,512]{1,0:T(8,128)(2,1)S(1)}, bf16[1024,512]{1,0:T(8,128)(2,1)S(1)}, u32[]{:S(2)}, u32[]{:S(2)}) %collective-permute-start.17) | collective-permute-done | bytes 1048608 | tf_op jit(solution)/shard_map/ppermute | solution.py:52
  112.4 12.5 %collective-permute-start.43 = (bf16[128,4096]{1,0:T(8,128)(2,1)S(1)}, bf16[128,4096]{1,0:T(8,128)(2,1)S(1)}, u32[]{:S(2)}, u32[]{:S(2)}) collective-permute-start(bf16[128,4096]{1,0:T(8,128)(2,1)S(1)} %copy-done.2), channel_id=1, source_target_pairs={{0,8},{8,16},{16,24},{1,9},{9,17},{17,25},{2,10},{10,18},{18,26},{... | collective-permute-start | bytes 3145736 | tf_op jit(solution)/shard_map/ppermute | solution.py:59
  125.6 18.5 %collective-permute-done.8 = bf16[512,512]{1,0:T(8,128)(2,1)S(1)} collective-permute-done((bf16[512,512]{1,0:T(8,128)(2,1)S(1)}, bf16[512,512]{1,0:T(8,128)(2,1)S(1)}, u32[]{:S(2)}, u32[]{:S(2)}) %collective-permute-start.8) | collective-permute-done | bytes 524320 | tf_op jit(solution)/shard_map/ppermute | solution.py:52
  148.5 31.3 %collective-permute-done.44 = bf16[128,4096]{1,0:T(8,128)(2,1)S(1)} collective-permute-done((bf16[128,4096]{1,0:T(8,128)(2,1)S(1)}, bf16[128,4096]{1,0:T(8,128)(2,1)S(1)}, u32[]{:S(2)}, u32[]{:S(2)}) %collective-permute-start.44) | collective-permute-done | bytes 1048608 | tf_op jit(solution)/shard_map/ppermute | solution.py:60
  182.6 8.0 %collective-permute-start.37 = (f32[128,1024]{1,0:T(8,128)S(1)}, f32[128,1024]{1,0:T(8,128)S(1)}, u32[]{:S(2)}, u32[]{:S(2)}) collective-permute-start(f32[128,1024]{1,0:T(8,128)S(1)} %get-tuple-element.50), channel_id=1, source_target_pairs={{0,8},{1,9},{2,10},{3,11},{4,12},{5,13},{6,14},{7,15}} | collective-permute-start | bytes 1572872 | tf_op jit(solution)/shard_map/ppermute | solution.py:48
  195.1 11.7 %collective-permute-done.45 = bf16[128,4096]{1,0:T(8,128)(2,1)S(1)} collective-permute-done((bf16[128,4096]{1,0:T(8,128)(2,1)S(1)}, bf16[128,4096]{1,0:T(8,128)(2,1)S(1)}, u32[]{:S(2)}, u32[]{:S(2)}) %collective-permute-start.45) | collective-permute-done | bytes 1048608 | tf_op jit(solution)/shard_map/ppermute | solution.py:60
  213.9 4.6 %collective-permute-start.10 = (f32[128,1024]{1,0:T(8,128)S(1)}, f32[128,1024]{1,0:T(8,128)S(1)}, u32[]{:S(2)}, u32[]{:S(2)}) collective-permute-start(f32[128,1024]{1,0:T(8,128)S(1)} %get-tuple-element.32), channel_id=1, source_target_pairs={{0,8},{1,9},{2,10},{3,11},{4,12},{5,13},{6,14},{7,15}} | collective-permute-start | bytes 1572872 | tf_op jit(solution)/shard_map/ppermute | solution.py:48
  219.4 5.7 %collective-permute-done.19 = f32[128,1024]{1,0:T(8,128)S(1)} collective-permute-done((f32[128,1024]{1,0:T(8,128)S(1)}, f32[128,1024]{1,0:T(8,128)S(1)}, u32[]{:S(2)}, u32[]{:S(2)}) %collective-permute-start.19) | collective-permute-done | bytes 524320 | tf_op jit(solution)/shard_map/ppermute | solution.py:48
  226.0 8.8 %collective-permute-done.10 = f32[128,1024]{1,0:T(8,128)S(1)} collective-permute-done((f32[128,1024]{1,0:T(8,128)S(1)}, f32[128,1024]{1,0:T(8,128)S(1)}, u32[]{:S(2)}, u32[]{:S(2)}) %collective-permute-start.10) | collective-permute-done | bytes 524320 | tf_op jit(solution)/shard_map/ppermute | solution.py:48
  247.4 8.9 %collective-permute-start.20 = (f32[128,1024]{1,0:T(8,128)S(1)}, f32[128,1024]{1,0:T(8,128)S(1)}, u32[]{:S(2)}, u32[]{:S(2)}) collective-permute-start(f32[128,1024]{1,0:T(8,128)S(1)} %get-tuple-element.36), channel_id=1, source_target_pairs={{0,8},{8,16},{1,9},{9,17},{2,10},{10,18},{3,11},{11,19},{4,12},{12... | collective-permute-start | bytes 1572872 | tf_op jit(solution)/shard_map/ppermute | solution.py:48
  258.0 7.8 %collective-permute-start.11 = (f32[128,1024]{1,0:T(8,128)S(1)}, f32[128,1024]{1,0:T(8,128)S(1)}, u32[]{:S(2)}, u32[]{:S(2)}) collective-permute-start(f32[128,1024]{1,0:T(8,128)S(1)} %get-tuple-element.30), channel_id=1, source_target_pairs={{0,8},{8,16},{1,9},{9,17},{2,10},{10,18},{3,11},{11,19},{4,12},{12... | collective-permute-start | bytes 1572872 | tf_op jit(solution)/shard_map/ppermute | solution.py:48
  268.2 5.7 %collective-permute-done.20 = f32[128,1024]{1,0:T(8,128)S(1)} collective-permute-done((f32[128,1024]{1,0:T(8,128)S(1)}, f32[128,1024]{1,0:T(8,128)S(1)}, u32[]{:S(2)}, u32[]{:S(2)}) %collective-permute-start.20) | collective-permute-done | bytes 524320 | tf_op jit(solution)/shard_map/ppermute | solution.py:48
  279.8 5.3 %collective-permute-done.11 = f32[128,1024]{1,0:T(8,128)S(1)} collective-permute-done((f32[128,1024]{1,0:T(8,128)S(1)}, f32[128,1024]{1,0:T(8,128)S(1)}, u32[]{:S(2)}, u32[]{:S(2)}) %collective-permute-start.11) | collective-permute-done | bytes 524320 | tf_op jit(solution)/shard_map/ppermute | solution.py:48
  286.6 9.0 %collective-permute-start.30 = (f32[128,1024]{1,0:T(8,128)S(1)}, f32[128,1024]{1,0:T(8,128)S(1)}, u32[]{:S(2)}, u32[]{:S(2)}) collective-permute-start(f32[128,1024]{1,0:T(8,128)S(1)} %get-tuple-element.40), channel_id=1, source_target_pairs={{0,8},{8,16},{16,24},{1,9},{9,17},{17,25},{2,10},{10,18},{18,26},{... | collective-permute-start | bytes 1572872 | tf_op jit(solution)/shard_map/ppermute | solution.py:48
  297.2 21.1 %collective-permute-start.21 = (f32[128,1024]{1,0:T(8,128)S(1)}, f32[128,1024]{1,0:T(8,128)S(1)}, u32[]{:S(2)}, u32[]{:S(2)}) collective-permute-start(f32[128,1024]{1,0:T(8,128)S(1)} %get-tuple-element.34), channel_id=1, source_target_pairs={{0,8},{8,16},{16,24},{1,9},{9,17},{17,25},{2,10},{10,18},{18,26},{... | collective-permute-start | bytes 1572872 | tf_op jit(solution)/shard_map/ppermute | solution.py:48
  319.8 9.8 %collective-permute-start.12 = (f32[128,1024]{1,0:T(8,128)S(1)}, f32[128,1024]{1,0:T(8,128)S(1)}, u32[]{:S(2)}, u32[]{:S(2)}) collective-permute-start(f32[128,1024]{1,0:T(8,128)S(1)} %get-tuple-element.28), channel_id=1, source_target_pairs={{0,8},{8,16},{16,24},{1,9},{9,17},{17,25},{2,10},{10,18},{18,26},{... | collective-permute-start | bytes 1572872 | tf_op jit(solution)/shard_map/ppermute | solution.py:48
  339.6 16.2 %collective-permute-done.55 = bf16[128,4096]{1,0:T(8,128)(2,1)S(1)} collective-permute-done((bf16[128,4096]{1,0:T(8,128)(2,1)S(1)}, bf16[128,4096]{1,0:T(8,128)(2,1)S(1)}, u32[]{:S(2)}, u32[]{:S(2)}) %collective-permute-start.55) | collective-permute-done | bytes 1048608 | tf_op jit(solution)/shard_map/ppermute | solution.py:52
  355.8 38.8 %collective-permute-done.59 = bf16[128,4096]{1,0:T(8,128)(2,1)S(1)} collective-permute-done((bf16[128,4096]{1,0:T(8,128)(2,1)S(1)}, bf16[128,4096]{1,0:T(8,128)(2,1)S(1)}, u32[]{:S(2)}, u32[]{:S(2)}) %collective-permute-start.59) | collective-permute-done | bytes 1048608 | tf_op jit(solution)/shard_map/ppermute | solution.py:52
  395.3 7.0 %fusion.68 = f32[4096,512]{1,0:T(8,128)} fusion(bf16[1024,4096]{1,0:T(8,128)(2,1)S(1)} %constant_dynamic-update-slice_fusion, bf16[1024,512]{1,0:T(8,128)(2,1)S(1)} %get-tuple-element.69), kind=kOutput, calls=%fused_computation.144 | convolution fusion | flops 4294967296 | bytes 17825792 | tf_op jit(solution)/shard_map/dot_general | solution.py:136
  407.0 8.6 %add_convert_fusion = bf16[4096,512]{1,0:T(8,128)(2,1)} fusion(f32[4096,512]{1,0:T(8,128)} %fusion.68, f32[4096,512]{1,0:T(8,128)} %fusion, bf16[128,4096]{1,0:T(8,128)(2,1)S(1)} %collective-permute-done.60, bf16[128,4096]{1,0:T(8,128)(2,1)S(1)} %collective-permute-done.59, bf16[128,4096]{1,0:T(8,128)(2,1)S(1)} %collective-permute-done.58, ...), kind=kOutput, calls=%fused_computation | convolution fusion | flops 2172649472 | bytes 25690112 | tf_op jit(solution)/shard_map/dot_general | solution.py:136
  (173 shorter events, 105.3 us)
Async XLA Ops:
  8.0 70.7 %collective-permute-start.35 = (bf16[1024,512]{1,0:T(8,128)(2,1)}, bf16[1024,512]{1,0:T(8,128)(2,1)}, u32[]{:S(2)}, u32[]{:S(2)}) collective-permute-start(bf16[1024,512]{1,0:T(8,128)(2,1)} %get-tuple-element.26), channel_id=1, source_target_pairs={{0,4},{2,6},{4,0},{6,2},{1,5},{3,7},{5,1},{7,3},{8,12},{10,14},{12... | collective-permute-start | bytes 3145736 | tf_op jit(solution)/shard_map/ppermute | solution.py:52
  9.5 82.8 %collective-permute-start.34 = (bf16[1024,512]{1,0:T(8,128)(2,1)}, bf16[1024,512]{1,0:T(8,128)(2,1)}, u32[]{:S(2)}, u32[]{:S(2)}) collective-permute-start(bf16[1024,512]{1,0:T(8,128)(2,1)} %get-tuple-element.26), channel_id=1, source_target_pairs={{0,2},{2,0},{4,6},{6,4},{1,3},{3,1},{5,7},{7,5},{8,10},{10,8},{12,... | collective-permute-start | bytes 3145736 | tf_op jit(solution)/shard_map/ppermute | solution.py:52
  32.3 36.0 %collective-permute-start.2 = (bf16[512,512]{1,0:T(8,128)(2,1)}, bf16[512,512]{1,0:T(8,128)(2,1)}, u32[]{:S(2)}, u32[]{:S(2)}) collective-permute-start(bf16[512,512]{1,0:T(8,128)(2,1)} %get-tuple-element.55), channel_id=1, source_target_pairs={{0,16},{8,24},{16,0},{24,8},{1,17},{9,25},{17,1},{25,9},{2,18},{10... | collective-permute-start | bytes 1572872 | tf_op jit(solution)/shard_map/ppermute | solution.py:43
  34.9 34.4 %collective-permute-start.3 = (bf16[512,512]{1,0:T(8,128)(2,1)}, bf16[512,512]{1,0:T(8,128)(2,1)}, u32[]{:S(2)}, u32[]{:S(2)}) collective-permute-start(bf16[512,512]{1,0:T(8,128)(2,1)} %get-tuple-element.56), channel_id=1, source_target_pairs={{0,24},{8,0},{16,8},{24,16},{1,25},{9,1},{17,9},{25,17},{2,26},{10... | collective-permute-start | bytes 1572872 | tf_op jit(solution)/shard_map/ppermute | solution.py:43
  47.5 43.4 %collective-permute-start.26 = (bf16[1024,512]{1,0:T(8,128)(2,1)S(1)}, bf16[1024,512]{1,0:T(8,128)(2,1)S(1)}, u32[]{:S(2)}, u32[]{:S(2)}) collective-permute-start(bf16[1024,512]{1,0:T(8,128)(2,1)S(1)} %copy-done.5), channel_id=1, source_target_pairs={{0,4},{2,6},{4,0},{6,2},{1,5},{3,7},{5,1},{7,3},{8,12},{10,14},{12... | collective-permute-start | bytes 3145736 | tf_op jit(solution)/shard_map/ppermute | solution.py:52
  79.1 32.3 %collective-permute-start.17 = (bf16[1024,512]{1,0:T(8,128)(2,1)S(1)}, bf16[1024,512]{1,0:T(8,128)(2,1)S(1)}, u32[]{:S(2)}, u32[]{:S(2)}) collective-permute-start(bf16[1024,512]{1,0:T(8,128)(2,1)S(1)} %copy-done.4), channel_id=1, source_target_pairs={{0,4},{2,6},{4,0},{6,2},{1,5},{3,7},{5,1},{7,3},{8,12},{10,14},{12... | collective-permute-start | bytes 3145736 | tf_op jit(solution)/shard_map/ppermute | solution.py:52
  92.3 54.3 %collective-permute-start.7 = (bf16[1024,512]{1,0:T(8,128)(2,1)S(1)}, bf16[1024,512]{1,0:T(8,128)(2,1)S(1)}, u32[]{:S(2)}, u32[]{:S(2)}) collective-permute-start(bf16[1024,512]{1,0:T(8,128)(2,1)S(1)} %copy-done.3), channel_id=1, source_target_pairs={{0,4},{2,6},{4,0},{6,2},{1,5},{3,7},{5,1},{7,3},{8,12},{10,14},{12... | collective-permute-start | bytes 3145736 | tf_op jit(solution)/shard_map/ppermute | solution.py:52
  93.8 51.7 %collective-permute-start.36 = (bf16[1024,512]{1,0:T(8,128)(2,1)}, bf16[1024,512]{1,0:T(8,128)(2,1)S(1)}, u32[]{:S(2)}, u32[]{:S(2)}) collective-permute-start(bf16[1024,512]{1,0:T(8,128)(2,1)} %collective-permute-done.35), channel_id=1, source_target_pairs={{0,2},{2,0},{4,6},{6,4},{1,3},{3,1},{5,7},{7,5},{8,10},{10,8},{12,... | collective-permute-start | bytes 3145736 | tf_op jit(solution)/shard_map/ppermute | solution.py:52
  95.8 95.5 %collective-permute-start.5 = (bf16[1024,512]{1,0:T(8,128)(2,1)S(1)}, bf16[1024,512]{1,0:T(8,128)(2,1)S(1)}, u32[]{:S(2)}, u32[]{:S(2)}) collective-permute-start(bf16[1024,512]{1,0:T(8,128)(2,1)S(1)} %copy-done.3), channel_id=1, source_target_pairs={{0,2},{2,0},{4,6},{6,4},{1,3},{3,1},{5,7},{7,5},{8,10},{10,8},{12,... | collective-permute-start | bytes 3145736 | tf_op jit(solution)/shard_map/ppermute | solution.py:52
  111.4 32.8 %collective-permute-start.8 = (bf16[512,512]{1,0:T(8,128)(2,1)S(1)}, bf16[512,512]{1,0:T(8,128)(2,1)S(1)}, u32[]{:S(2)}, u32[]{:S(2)}) collective-permute-start(bf16[512,512]{1,0:T(8,128)(2,1)S(1)} %pad_maximum_fusion.4), channel_id=1, source_target_pairs={{0,6},{2,4},{4,2},{6,0},{1,7},{3,5},{5,3},{7,1},{8,14},{10,12},{12... | collective-permute-start | bytes 1572872 | tf_op jit(solution)/shard_map/ppermute | solution.py:52
  112.4 35.4 %collective-permute-start.43 = (bf16[128,4096]{1,0:T(8,128)(2,1)S(1)}, bf16[128,4096]{1,0:T(8,128)(2,1)S(1)}, u32[]{:S(2)}, u32[]{:S(2)}) collective-permute-start(bf16[128,4096]{1,0:T(8,128)(2,1)S(1)} %copy-done.2), channel_id=1, source_target_pairs={{0,8},{8,16},{16,24},{1,9},{9,17},{17,25},{2,10},{10,18},{18,26},{... | collective-permute-start | bytes 3145736 | tf_op jit(solution)/shard_map/ppermute | solution.py:59
  144.2 35.6 %collective-permute-start.44 = (bf16[128,4096]{1,0:T(8,128)(2,1)S(1)}, bf16[128,4096]{1,0:T(8,128)(2,1)S(1)}, u32[]{:S(2)}, u32[]{:S(2)}) collective-permute-start(bf16[128,4096]{1,0:T(8,128)(2,1)S(1)} %copy-done.2), channel_id=1, source_target_pairs={{24,16},{16,8},{8,0},{25,17},{17,9},{9,1},{26,18},{18,10},{10,2},{... | collective-permute-start | bytes 3145736 | tf_op jit(solution)/shard_map/ppermute | solution.py:60
  145.5 35.6 %collective-permute-start.27 = (bf16[1024,512]{1,0:T(8,128)(2,1)S(1)}, bf16[1024,512]{1,0:T(8,128)(2,1)S(1)}, u32[]{:S(2)}, u32[]{:S(2)}) collective-permute-start(bf16[1024,512]{1,0:T(8,128)(2,1)S(1)} %collective-permute-done.26), channel_id=1, source_target_pairs={{0,2},{2,0},{4,6},{6,4},{1,3},{3,1},{5,7},{7,5},{8,10},{10,8},{12,... | collective-permute-start | bytes 3145736 | tf_op jit(solution)/shard_map/ppermute | solution.py:52
  146.6 36.0 %collective-permute-start.18 = (bf16[1024,512]{1,0:T(8,128)(2,1)S(1)}, bf16[1024,512]{1,0:T(8,128)(2,1)S(1)}, u32[]{:S(2)}, u32[]{:S(2)}) collective-permute-start(bf16[1024,512]{1,0:T(8,128)(2,1)S(1)} %collective-permute-done.17), channel_id=1, source_target_pairs={{0,2},{2,0},{4,6},{6,4},{1,3},{3,1},{5,7},{7,5},{8,10},{10,8},{12,... | collective-permute-start | bytes 3145736 | tf_op jit(solution)/shard_map/ppermute | solution.py:52
  147.8 45.1 %collective-permute-start.9 = (bf16[1024,512]{1,0:T(8,128)(2,1)S(1)}, bf16[1024,512]{1,0:T(8,128)(2,1)S(1)}, u32[]{:S(2)}, u32[]{:S(2)}) collective-permute-start(bf16[1024,512]{1,0:T(8,128)(2,1)S(1)} %collective-permute-done.7), channel_id=1, source_target_pairs={{0,2},{2,0},{4,6},{6,4},{1,3},{3,1},{5,7},{7,5},{8,10},{10,8},{12,... | collective-permute-start | bytes 3145736 | tf_op jit(solution)/shard_map/ppermute | solution.py:52
  285.1 46.2 %collective-permute-start.53 = (bf16[128,4096]{1,0:T(8,128)(2,1)S(1)}, bf16[128,4096]{1,0:T(8,128)(2,1)S(1)}, u32[]{:S(2)}, u32[]{:S(2)}) collective-permute-start(bf16[128,4096]{1,0:T(8,128)(2,1)S(1)} %copy-done.2), channel_id=1, source_target_pairs={{0,4},{2,6},{4,0},{6,2},{1,5},{3,7},{5,1},{7,3},{8,12},{10,14},{12... | collective-permute-start | bytes 3145736 | tf_op jit(solution)/shard_map/ppermute | solution.py:52
  286.6 31.9 %collective-permute-start.30 = (f32[128,1024]{1,0:T(8,128)S(1)}, f32[128,1024]{1,0:T(8,128)S(1)}, u32[]{:S(2)}, u32[]{:S(2)}) collective-permute-start(f32[128,1024]{1,0:T(8,128)S(1)} %get-tuple-element.40), channel_id=1, source_target_pairs={{0,8},{8,16},{16,24},{1,9},{9,17},{17,25},{2,10},{10,18},{18,26},{... | collective-permute-start | bytes 1572872 | tf_op jit(solution)/shard_map/ppermute | solution.py:48
  297.1 40.7 %collective-permute-start.50 = (bf16[128,4096]{1,0:T(8,128)(2,1)S(1)}, bf16[128,4096]{1,0:T(8,128)(2,1)S(1)}, u32[]{:S(2)}, u32[]{:S(2)}) collective-permute-start(bf16[128,4096]{1,0:T(8,128)(2,1)S(1)} %get-tuple-element.23), channel_id=1, source_target_pairs={{0,2},{2,0},{4,6},{6,4},{1,3},{3,1},{5,7},{7,5},{8,10},{10,8},{12,... | collective-permute-start | bytes 3145736 | tf_op jit(solution)/shard_map/ppermute | solution.py:52
  297.2 32.5 %collective-permute-start.21 = (f32[128,1024]{1,0:T(8,128)S(1)}, f32[128,1024]{1,0:T(8,128)S(1)}, u32[]{:S(2)}, u32[]{:S(2)}) collective-permute-start(f32[128,1024]{1,0:T(8,128)S(1)} %get-tuple-element.34), channel_id=1, source_target_pairs={{0,8},{8,16},{16,24},{1,9},{9,17},{17,25},{2,10},{10,18},{18,26},{... | collective-permute-start | bytes 1572872 | tf_op jit(solution)/shard_map/ppermute | solution.py:48
  331.4 63.2 %collective-permute-start.57 = (bf16[128,4096]{1,0:T(8,128)(2,1)S(1)}, bf16[128,4096]{1,0:T(8,128)(2,1)S(1)}, u32[]{:S(2)}, u32[]{:S(2)}) collective-permute-start(bf16[128,4096]{1,0:T(8,128)(2,1)S(1)} %get-tuple-element.21), channel_id=1, source_target_pairs={{0,4},{2,6},{4,0},{6,2},{1,5},{3,7},{5,1},{7,3},{8,12},{10,14},{12... | collective-permute-start | bytes 3145736 | tf_op jit(solution)/shard_map/ppermute | solution.py:52
  336.3 58.4 %collective-permute-start.59 = (bf16[128,4096]{1,0:T(8,128)(2,1)S(1)}, bf16[128,4096]{1,0:T(8,128)(2,1)S(1)}, u32[]{:S(2)}, u32[]{:S(2)}) collective-permute-start(bf16[128,4096]{1,0:T(8,128)(2,1)S(1)} %get-tuple-element.19), channel_id=1, source_target_pairs={{0,4},{2,6},{4,0},{6,2},{1,5},{3,7},{5,1},{7,3},{8,12},{10,14},{12... | collective-permute-start | bytes 3145736 | tf_op jit(solution)/shard_map/ppermute | solution.py:52
  337.8 57.4 %collective-permute-start.52 = (bf16[128,4096]{1,0:T(8,128)(2,1)S(1)}, bf16[128,4096]{1,0:T(8,128)(2,1)S(1)}, u32[]{:S(2)}, u32[]{:S(2)}) collective-permute-start(bf16[128,4096]{1,0:T(8,128)(2,1)S(1)} %get-tuple-element.19), channel_id=1, source_target_pairs={{0,2},{2,0},{4,6},{6,4},{1,3},{3,1},{5,7},{7,5},{8,10},{10,8},{12,... | collective-permute-start | bytes 3145736 | tf_op jit(solution)/shard_map/ppermute | solution.py:52
  339.1 63.2 %collective-permute-start.54 = (bf16[128,4096]{1,0:T(8,128)(2,1)S(1)}, bf16[128,4096]{1,0:T(8,128)(2,1)S(1)}, u32[]{:S(2)}, u32[]{:S(2)}) collective-permute-start(bf16[128,4096]{1,0:T(8,128)(2,1)S(1)} %collective-permute-done.53), channel_id=1, source_target_pairs={{0,2},{2,0},{4,6},{6,4},{1,3},{3,1},{5,7},{7,5},{8,10},{10,8},{12,... | collective-permute-start | bytes 3145736 | tf_op jit(solution)/shard_map/ppermute | solution.py:52
  355.8 46.5 %collective-permute-start.56 = (bf16[128,4096]{1,0:T(8,128)(2,1)S(1)}, bf16[128,4096]{1,0:T(8,128)(2,1)S(1)}, u32[]{:S(2)}, u32[]{:S(2)}) collective-permute-start(bf16[128,4096]{1,0:T(8,128)(2,1)S(1)} %collective-permute-done.55), channel_id=1, source_target_pairs={{0,2},{2,0},{4,6},{6,4},{1,3},{3,1},{5,7},{7,5},{8,10},{10,8},{12,... | collective-permute-start | bytes 3145736 | tf_op jit(solution)/shard_map/ppermute | solution.py:52
  (45 other events, 911.8 us)
